TPU v7x, 32 devices: a whole 2x2x4 slice. The times are simulated.
32 devices in a mesh: gz: 4 (over x, core), gx: 4 (over z), gy: 2 (over y).
Axes of the slice: x: 2, y: 2, z: 4, core: 2. Of those that a mesh axis runs over, the one named last changes fastest.
Arguments:
- offsets: float32 [3, 4, 8, 8, 128], P(None, 'gz', 'gx', 'gy'), may hold values from 0 to 10
- type_ids: int32 [4, 8, 8, 128], P('gz', 'gx', 'gy'), may hold values from 0 to 2
- occupied: int32 [4, 8, 8, 128], P('gz', 'gx', 'gy'), may hold values from 0 to 1, as said below
- prior_charges: float32 [2, 4, 8, 8, 128], P(None, 'gz', 'gx', 'gy'), may hold values from -0.6 to 0.6
- electronegativity: float32 [3], replicated, may hold values from 2 to 10
- hardness: float32 [3], replicated, may hold values from 4 to 12
- shielding: float32 [3], replicated, may hold values from 0.5 to 1.2
Outputs:
- charges: float32 [4, 8, 8, 128], P('gz', 'gx', 'gy')
- residuals: float32 [2, 4, 8, 8, 128], P(None, 'gz', 'gx', 'gy')
Inputs may be any that keep to these rules, and one draw needn't show every extreme that they name: `occupied`: 1 marks a slot that holds an atom, 0 a padding slot.
All inputs are finite; a program needn't handle non-finite values.
Results may differ from a plain program's by a relative error of at most 0.00021.
Values sent between devices are 32-bit elements; how exact they have to be, the bound alone decides.
A program may use at most 128 MiB of HBM per device.

v0:
```python
import functools

import jax
import jax.numpy as jnp
from jax import lax
from jax.experimental import pallas as pl
from jax.experimental.pallas import tpu as pltpu
from jax.sharding import PartitionSpec as P

ITERS = 4
AXES = ("gz", "gx", "gy")
MESH = pl.DeviceIdType.MESH

coulomb_factor = 14.4
cell_edge = 10.0
CHUNK = 64


def kernel(
    sizes, dys,
    offsets, type_ids, occupied, prior, electro, hardness, shielding,
    charges, residuals,
    first, fields, pair, local, sums, parts, mine,
    send_sem, recv_sem, part_send, part_recv,
):
    nz, nx, ny = sizes
    cells_x, cells_y, slots = type_ids.shape[1:]
    rows = 2 * cells_y
    geo_rows = 4 * cells_y
    cells = cells_x * cells_y
    devices = nz * nx * ny
    me_z, me_x, me_y = (lax.axis_index(name) for name in AXES)

    at_x = [lax.rem(me_x + d, nx) for d in range(nx)]
    at_y = [lax.rem(me_y + d, ny) for d in range(ny)]

    def each_peer(action):
        def layer(dz, skip):
            z = lax.rem(me_z + dz, nz)
            for dx in range(nx):
                for dy in range(ny):
                    if not (skip and dx == 0 and dy == 0):
                        action((z, at_x[dx], at_y[dy]), (dz * nx + dx) * ny + dy - 1)

        layer(0, True)
        if nz <= 4:
            for dz in range(1, nz):
                layer(dz, False)
        else:
            pl.loop(1, nz)(lambda dz: layer(dz, False))

    barrier = pltpu.get_barrier_semaphore()
    each_peer(
        lambda peer, slot: pl.semaphore_signal(
            barrier, inc=1, device_id=peer, device_id_type=MESH
        )
    )

    def per_atom(table, ids):
        summed = jnp.zeros(ids.shape, jnp.float32)
        for species in range(table.shape[0]):
            summed = summed + jnp.where(ids == species, table[species], 0.0)
        return summed

    occ, stiff, rhs, x = [], [], [], []
    for i in range(cells_x):
        ids = type_ids[0, i]
        occ_i = occupied[0, i].astype(jnp.float32)
        radius = per_atom(shielding, ids) * (1.0 / cell_edge)
        for c in range(3):
            first[1, 0, i + 1, c * cells_y : (c + 1) * cells_y] = offsets[c, 0, i] * (
                1.0 / cell_edge
            )
        first[1, 0, i + 1, 3 * cells_y : geo_rows] = radius * radius
        stiff_i = per_atom(hardness, ids)
        affinity = per_atom(electro, ids)
        occ.append(jnp.concatenate([occ_i, occ_i], axis=0))
        stiff.append(jnp.concatenate([stiff_i, stiff_i], axis=0))
        rhs.append(jnp.concatenate([-affinity * occ_i, -occ_i], axis=0))
        start = jnp.concatenate([prior[0, 0, i] * occ_i, prior[1, 0, i] * occ_i], axis=0)
        x.append(start)
        first[1, 0, i + 1, geo_rows:] = start

    for edge, slot in ((0, 0), (nz - 1, 2)):

        @pl.when(me_z == edge)
        def _():
            first[slot] = jnp.zeros(first.shape[1:], jnp.float32)
            for k in range(ITERS):
                fields[k, slot] = jnp.zeros(fields.shape[2:], jnp.float32)

    messages = [
        (dz, dx, dy)
        for dz in (0, 1, -1)
        for dx in (0, 1, -1)
        for dy in dys
        if (dz, dx, dy) != (0, 0, 0)
    ]
    turn_x = {d: lax.rem(me_x + d + nx, nx) for d in (0, 1, -1)}
    turn_y = {d: lax.rem(me_y + d + ny, ny) for d in (0, 1, -1)}

    def copies(stage, buffer, action):
        for m, (dz, dx, dy) in enumerate(messages):
            source, target = {
                0: (pl.ds(1, cells_x), pl.ds(1, cells_x)),
                1: (pl.ds(cells_x, 1), pl.ds(0, 1)),
                -1: (pl.ds(1, 1), pl.ds(cells_x + 1, 1)),
            }[dx]
            copy = pltpu.make_async_remote_copy(
                src_ref=buffer.at[1, 0, source],
                dst_ref=buffer.at[1 - dz, dys.index(dy), target],
                send_sem=send_sem.at[stage, m],
                recv_sem=recv_sem.at[stage, m],
                device_id=(me_z + dz, turn_x[dx], turn_y[dy]),
                device_id_type=MESH,
            )
            action(copy, dz)

    def send(stage, buffer):
        def go(copy, dz):
            if dz == 0:
                copy.start()
            else:
                pl.when((me_z + dz >= 0) & (me_z + dz < nz))(copy.start)

        copies(stage, buffer, go)

    def receive(stage, buffer):
        def go(copy, dz):
            if dz == 0:
                copy.wait_recv()
            else:
                pl.when((me_z - dz >= 0) & (me_z - dz < nz))(copy.wait_recv)

        copies(stage, buffer, go)

    def sent(stage, buffer):
        def go(copy, dz):
            if dz == 0:
                copy.wait_send()
            else:
                pl.when((me_z + dz >= 0) & (me_z + dz < nz))(copy.wait_send)

        copies(stage, buffer, go)

    pl.semaphore_wait(barrier, devices - 1)
    send(0, first)

    shape = (slots, slots)
    eye = lax.broadcasted_iota(jnp.int32, shape, 0) == lax.broadcasted_iota(jnp.int32, shape, 1)

    @pl.loop(0, cells)
    def _(cell):
        i, j = cell // cells_y, cell % cells_y
        for c in range(4):
            row = first[1, 0, i + 1, pl.ds(c * cells_y + j, 1), :]
            column = jnp.sum(jnp.where(eye, row, 0.0), axis=1, keepdims=True)
            local[cell, c] = jnp.broadcast_to(column, shape)

    def beside(j, dy):
        y = j + dy
        if dy == 0:
            return 0, y
        if dy < 0:
            out = y < 0
            return jnp.where(out, 1, 0), jnp.where(out, y + cells_y, y)
        out = y >= cells_y
        return jnp.where(out, len(dys) - 1, 0), jnp.where(out, y - cells_y, y)

    def build():
        @pl.loop(0, cells)
        def _(cell):
            i, j = cell // cells_y, cell % cells_y
            where = [beside(j, dy) for dy in (-1, 0, 1)]

            @pl.loop(0, 9)
            def _(plane):
                dz, dx = plane // 3, plane % 3
                shift_z = (dz - 1).astype(jnp.float32)
                shift_x = (dx - 1).astype(jnp.float32)
                for k in range(3):
                    side, y = where[k]
                    tile = first.at[dz, side, i + dx]
                    bz = tile[pl.ds(y, 1), :] + shift_z
                    bx = tile[pl.ds(cells_y + y, 1), :] + shift_x
                    by = tile[pl.ds(2 * cells_y + y, 1), :] + (k - 1.0)
                    bs = tile[pl.ds(3 * cells_y + y, 1), :]
                    for part in range(slots // CHUNK):
                        span = pl.ds(part * CHUNK, CHUNK)
                        ez = bz - local[cell, 0, span]
                        ex = bx - local[cell, 1, span]
                        ey = by - local[cell, 2, span]
                        squared = ez * ez + ex * ex + ey * ey
                        fraction = squared * lax.rsqrt(jnp.maximum(squared, 1e-30))
                        reach = jnp.maximum(1.0 - fraction, 0.0)
                        reach = reach * reach
                        factor = coulomb_factor / cell_edge
                        taper = reach * reach * (4.0 * factor * fraction + factor)
                        pair[cell, plane * 3 + k, span] = taper * lax.rsqrt(
                            squared + (local[cell, 3, span] + bs)
                        )

    def operate(buffer, base, field):
        @pl.loop(0, cells)
        def _(cell):
            i, j = cell // cells_y, cell % cells_y
            where = [beside(j, dy) for dy in (-1, 0, 1)]
            total = [jnp.zeros(shape, jnp.float32) for _ in range(2)]
            for dz in range(3):
                for dx in range(3):
                    for k in range(3):
                        side, y = where[k]
                        tile = buffer.at[dz, side, i + dx]
                        block = pair[cell, (dz * 3 + dx) * 3 + k]
                        for s in range(2):
                            total[s] = total[s] + block * tile[
                                pl.ds(base + s * cells_y + y, 1), :
                            ]
            for s in range(2):
                sums[i, s * cells_y + j] = total[s]

        out = []
        for i in range(cells_x):
            lines = []
            for row in range(rows):
                column = jnp.sum(sums[i, row], axis=1, keepdims=True)
                lines.append(jnp.sum(jnp.where(eye, column, 0.0), axis=0, keepdims=True))
            out.append(occ[i] * (stiff[i] * field[i] + jnp.concatenate(lines, axis=0)))
        return out

    tile_shape = (rows, slots)
    lane = lax.broadcasted_iota(jnp.int32, tile_shape, 1)
    second = lax.broadcasted_iota(jnp.int32, tile_shape, 0) >= cells_y
    slot_of = lane - jnp.where(second, 8, 0)

    def part_copy(stage, peer, slot):
        return pltpu.make_async_remote_copy(
            src_ref=mine.at[stage],
            dst_ref=parts.at[stage, slot],
            send_sem=part_send.at[stage],
            recv_sem=part_recv.at[stage],
            device_id=peer,
            device_id_type=MESH,
        )

    def start_sums(stage, quantities):
        packed = jnp.zeros(tile_shape, jnp.float32)
        for k, quantity in enumerate(quantities):
            column = jnp.sum(functools.reduce(jnp.add, quantity), axis=1, keepdims=True)
            packed = jnp.where(slot_of == k, column, packed)
        mine[stage] = jnp.sum(packed, axis=0, keepdims=True)
        each_peer(lambda peer, slot: part_copy(stage, peer, slot).start())

    def finish_sums(stage, count):
        everything = parts.at[stage]
        pltpu.make_async_copy(everything, everything, part_recv.at[stage]).wait()
        row = mine[stage] + jnp.sum(parts[stage], axis=0)
        pltpu.make_async_copy(everything, everything, part_send.at[stage]).wait()
        return [
            jnp.where(
                second,
                jnp.broadcast_to(row[:, 8 + k : 9 + k], tile_shape),
                jnp.broadcast_to(row[:, k : k + 1], tile_shape),
            )
            for k in range(count)
        ]

    span = range(cells_x)

    def exchange_and_operate(stage, field):
        buffer = fields.at[stage - 1]
        for i in span:
            buffer[1, 0, i + 1] = field[i]
        send(stage, buffer)
        receive(stage, buffer)
        out = operate(buffer, 0, field)
        sent(stage, buffer)
        return out

    receive(0, first)
    build()
    image = operate(first, geo_rows, x)
    sent(0, first)
    r = [rhs[i] - image[i] for i in span]
    w = exchange_and_operate(1, r)

    p = s = z = None
    for stage in range(ITERS):
        quantities = [[r[i] * r[i] for i in span], [w[i] * r[i] for i in span]]
        last = stage == ITERS - 1
        if last:
            quantities += [x, r, p]
        start_sums(stage, quantities)
        n = None if last else exchange_and_operate(stage + 2, w)
        found = finish_sums(stage, len(quantities))
        gamma, delta = found[:2]
        if stage == 0:
            beta = None
            alpha = gamma / delta
            p, s, z = r, w, n
        else:
            beta = gamma / gamma_before
            alpha = gamma / (delta - beta * gamma / alpha)
            p = [r[i] + beta * p[i] for i in span]
            s = [w[i] + beta * s[i] for i in span]
            if not last:
                z = [n[i] + beta * z[i] for i in span]
        gamma_before = gamma
        x = [x[i] + alpha * p[i] for i in span]
        r = [r[i] - alpha * s[i] for i in span]
        if not last:
            w = [w[i] - alpha * z[i] for i in span]
    totals = found[2] + alpha * (found[3] + beta * found[4])
    ratio = totals[:cells_y] / totals[cells_y:]
    for i in span:
        charges[0, i] = x[i][:cells_y] - ratio * x[i][cells_y:]
        residuals[0, 0, i] = r[i][:cells_y]
        residuals[1, 0, i] = r[i][cells_y:]


def per_device(sizes, *arrays):
    type_ids = arrays[1]
    cells_x, cells_y, slots = type_ids.shape[1:]
    cells = cells_x * cells_y
    rows = 2 * cells_y
    devices = sizes[0] * sizes[1] * sizes[2]
    dys = (0, 1) if sizes[2] == 2 else (0, 1, -1)
    messages = 9 * len(dys) - 1
    halo = (3, len(dys), cells_x + 2)
    vmem = pl.BlockSpec(memory_space=pltpu.VMEM)
    smem = pl.BlockSpec(memory_space=pltpu.SMEM)
    return pl.pallas_call(
        functools.partial(kernel, sizes, dys),
        out_shape=(
            jax.ShapeDtypeStruct(type_ids.shape, jnp.float32),
            jax.ShapeDtypeStruct((2,) + type_ids.shape, jnp.float32),
        ),
        in_specs=[vmem] * 4 + [smem] * 3,
        out_specs=(vmem, vmem),
        scratch_shapes=[
            pltpu.VMEM(halo + (6 * cells_y, slots), jnp.float32),
            pltpu.VMEM((ITERS,) + halo + (rows, slots), jnp.float32),
            pltpu.VMEM((cells, 27, slots, slots), jnp.float32),
            pltpu.VMEM((cells, 4, slots, slots), jnp.float32),
            pltpu.VMEM((cells_x, rows, slots, slots), jnp.float32),
            pltpu.VMEM((ITERS, devices - 1, 1, slots), jnp.float32),
            pltpu.VMEM((ITERS, 1, slots), jnp.float32),
            pltpu.SemaphoreType.DMA((ITERS + 1, messages)),
            pltpu.SemaphoreType.DMA((ITERS + 1, messages)),
            pltpu.SemaphoreType.DMA((ITERS,)),
            pltpu.SemaphoreType.DMA((ITERS,)),
        ],
        compiler_params=pltpu.CompilerParams(
            collective_id=0, has_side_effects=True, vmem_limit_bytes=48 * 1024 * 1024
        ),
    )(*arrays)


def solution(mesh):
    sizes = tuple(mesh.shape[name] for name in AXES)
    in_specs = (
        P(None, "gz", "gx", "gy", None),
        P("gz", "gx", "gy", None),
        P("gz", "gx", "gy", None),
        P(None, "gz", "gx", "gy", None),
        P(),
        P(),
        P(),
    )
    out_specs = (P("gz", "gx", "gy", None), P(None, "gz", "gx", "gy", None))
    return jax.shard_map(
        functools.partial(per_device, sizes),
        mesh=mesh,
        in_specs=in_specs,
        out_specs=out_specs,
        check_vma=False,
    )
```

profile of v0, /device:TPU:0, one launch (start us, length us, event | category | flops | bytes accessed | tf_op | source)
XLA Modules:
  0.0 68.9 jit_solution(18314083260695474919)
XLA Ops:
  0.6 0.0 copy-start
  0.6 0.7 %copy-done = f32[3,1,2,4,128]{4,3,2,1,0:T(4,128)S(1)} copy-done((f32[3,1,2,4,128]{4,3,2,1,0:T(4,128)S(1)}, f32[3,1,2,4,128]{4,3,2,1,0:T(4,128)}, u32[]{:S(2)}) %copy-start) | copy-done | bytes 12312
  1.3 0.0 copy-start.1
  1.3 0.7 %copy-done.1 = f32[2,1,2,4,128]{4,3,2,1,0:T(4,128)S(1)} copy-done((f32[2,1,2,4,128]{4,3,2,1,0:T(4,128)S(1)}, f32[2,1,2,4,128]{4,3,2,1,0:T(4,128)}, u32[]{:S(2)}) %copy-start.1) | copy-done | bytes 8216
  2.0 0.0 copy-start.2
  2.0 0.7 copy-done.2
  2.7 0.0 copy-start.3
  2.7 0.7 copy-done.3
  3.4 0.0 copy-start.4
  3.4 0.7 copy-done.4
  4.1 0.0 copy-start.5
  4.1 0.7 copy-done.5
  4.7 0.0 copy-start.6
  4.7 0.7 copy-done.6
  5.4 62.3 %shard_map.86 = (f32[1,2,4,128]{3,2,1,0:T(4,128)S(1)}, f32[2,1,2,4,128]{4,3,2,1,0:T(4,128)S(1)}) custom-call(f32[3,1,2,4,128]{4,3,2,1,0:T(4,128)S(1)} %copy-done, s32[1,2,4,128]{3,2,1,0:T(4,128)S(1)} %copy-done.2, s32[1,2,4,128]{3,2,1,0:T(4,128)S(1)} %copy-done.3, f32[2,1,2,4,128]{4,3,2,1,0:T(4,128)S(1)} %copy-done.1, f32[3]{0:T(128)S(1)} %copy-done.4, ...), custom_call_target="tpu_custom_call" | custom-call | tf_op jit(solution)/shard_map/pallas_call | solution.py:332
  67.7 0.6 copy.11
  68.3 0.6 copy.12
Async XLA Ops:
  0.6 0.7 %copy-start = (f32[3,1,2,4,128]{4,3,2,1,0:T(4,128)S(1)}, f32[3,1,2,4,128]{4,3,2,1,0:T(4,128)}, u32[]{:S(2)}) copy-start(f32[3,1,2,4,128]{4,3,2,1,0:T(4,128)} %offsets.1) | copy-start | bytes 36868
  1.3 0.7 %copy-start.1 = (f32[2,1,2,4,128]{4,3,2,1,0:T(4,128)S(1)}, f32[2,1,2,4,128]{4,3,2,1,0:T(4,128)}, u32[]{:S(2)}) copy-start(f32[2,1,2,4,128]{4,3,2,1,0:T(4,128)} %prior.1) | copy-start | bytes 24580
  2.0 0.7 copy-start.2
  2.7 0.7 copy-start.3
  3.4 0.7 copy-start.4
  4.1 0.7 copy-start.5
  4.7 0.7 copy-start.6
where the time goes:
time: 69.3 us; the launch traced here: 68.9 us
  Pallas kernels  62.3 us (90%)
  local copies, waits for them, and re-layouts  5.93 us (9%)
    pallas_call x1, Pallas kernels, per_device(): pl.pallas_call(functools.partial(kernel, sizes, dys), out_shape=(jax.Shap...  62.3 us
    unnamed x16, local copies, waits for them, and re-layouts  5.93 us

commit v1 on v0

v1 whole, which is shorter than its diff:
```python
import functools

import jax
import jax.numpy as jnp
from jax import lax
from jax.experimental import pallas as pl
from jax.experimental.pallas import tpu as pltpu
from jax.sharding import PartitionSpec as P

ITERS = 4
AXES = ("gz", "gx", "gy")
MESH = pl.DeviceIdType.MESH

coulomb_factor = 14.4
cell_edge = 10.0
CHUNK = 64


def kernel(
    sizes, dys,
    offsets_in, type_ids_in, occupied_in, prior_in, electro_in, hardness_in, shielding_in,
    charges, residuals,
    offsets, type_ids, occupied, prior, electro, hardness, shielding,
    first, fields, first_edge, edges, pair, local, sums, parts, mine,
    in_sem, send_sem, recv_sem, part_send, part_recv,
):
    loads = [
        pltpu.make_async_copy(source, target, in_sem.at[k])
        for k, (source, target) in enumerate(
            zip(
                (offsets_in, type_ids_in, occupied_in, prior_in,
                 electro_in, hardness_in, shielding_in),
                (offsets, type_ids, occupied, prior, electro, hardness, shielding),
            )
        )
    ]
    for load in loads:
        load.start()
    nz, nx, ny = sizes
    cells_x, cells_y, slots = type_ids.shape[1:]
    rows = 2 * cells_y
    geo_rows = 4 * cells_y
    cells = cells_x * cells_y
    devices = nz * nx * ny
    sides = len(dys) - 1
    me_z, me_x, me_y = (lax.axis_index(name) for name in AXES)

    at_x = [lax.rem(me_x + d, nx) for d in range(nx)]
    at_y = [lax.rem(me_y + d, ny) for d in range(ny)]

    def each_peer(action):
        def layer(dz, skip):
            z = lax.rem(me_z + dz, nz)
            for dx in range(nx):
                for dy in range(ny):
                    if not (skip and dx == 0 and dy == 0):
                        action((z, at_x[dx], at_y[dy]), (dz * nx + dx) * ny + dy - 1)

        layer(0, True)
        if nz <= 4:
            for dz in range(1, nz):
                layer(dz, False)
        else:
            pl.loop(1, nz)(lambda dz: layer(dz, False))

    barrier = pltpu.get_barrier_semaphore()
    each_peer(
        lambda peer, slot: pl.semaphore_signal(
            barrier, inc=1, device_id=peer, device_id_type=MESH
        )
    )

    def per_atom(table, ids):
        summed = jnp.zeros(ids.shape, jnp.float32)
        for species in range(table.shape[0]):
            summed = summed + jnp.where(ids == species, table[species], 0.0)
        return summed

    for load in loads:
        load.wait()
    occ, stiff, rhs, x = [], [], [], []

    def ends(values):
        return [values[:1], values[cells_y - 1 : cells_y]]

    for i in range(cells_x):
        ids = type_ids[0, i]
        occ_i = occupied[0, i].astype(jnp.float32)
        radius = per_atom(shielding, ids) * (1.0 / cell_edge)
        geo = [offsets[c, 0, i] * (1.0 / cell_edge) for c in range(3)] + [radius * radius]
        first[1, i + 1, :geo_rows] = jnp.concatenate(geo, axis=0)
        stiff_i = per_atom(hardness, ids)
        affinity = per_atom(electro, ids)
        occ.append(jnp.concatenate([occ_i, occ_i], axis=0))
        stiff.append(jnp.concatenate([stiff_i, stiff_i], axis=0))
        rhs.append(jnp.concatenate([-affinity * occ_i, -occ_i], axis=0))
        start = jnp.concatenate([prior[0, 0, i] * occ_i, prior[1, 0, i] * occ_i], axis=0)
        x.append(start)
        first[1, i + 1, geo_rows : geo_rows + rows] = start
        pieces = geo + [start[:cells_y], start[cells_y:]]
        first_edge[i] = jnp.concatenate([end for v in pieces for end in ends(v)], axis=0)

    for edge, slot in ((0, 0), (nz - 1, 2)):

        @pl.when(me_z == edge)
        def _():
            first[slot] = jnp.zeros(first.shape[1:], jnp.float32)
            for k in range(ITERS):
                fields[k, slot] = jnp.zeros(fields.shape[2:], jnp.float32)

    messages = [
        (dz, dx, dy)
        for dz in (1, -1, 0)
        for dx in (1, -1, 0)
        for dy in reversed(dys)
        if (dz, dx, dy) != (0, 0, 0)
    ]
    turn_x = {d: lax.rem(me_x + d + nx, nx) for d in (0, 1, -1)}
    turn_y = {d: lax.rem(me_y + d + ny, ny) for d in (0, 1, -1)}

    def copies(stage, buffer, edge, own_rows, action, layers=(1, -1, 0)):
        edge_rows = edge.shape[1]
        for m, (dz, dx, dy) in enumerate(messages):
            if dz not in layers:
                continue
            source, target, count = {
                0: (0, 1, cells_x),
                1: (cells_x - 1, 0, 1),
                -1: (0, cells_x + 1, 1),
            }[dx]
            if dy == 0:
                src = buffer.at[1, pl.ds(source + 1, count), pl.ds(0, own_rows)]
                span = pl.ds(0, own_rows)
            else:
                src = edge.at[pl.ds(source, count)]
                span = pl.ds(own_rows + (dys.index(dy) - 1) * edge_rows, edge_rows)
            copy = pltpu.make_async_remote_copy(
                src_ref=src,
                dst_ref=buffer.at[1 - dz, pl.ds(target, count), span],
                send_sem=send_sem.at[stage, m],
                recv_sem=recv_sem.at[stage, m],
                device_id=(me_z + dz, turn_x[dx], turn_y[dy]),
                device_id_type=MESH,
            )
            action(copy, dz)

    def guarded(name, sign):
        def go(copy, dz):
            act = getattr(copy, name)
            if dz == 0:
                act()
            else:
                other = me_z + sign * dz
                pl.when((other >= 0) & (other < nz))(act)

        return go

    def send(*what):
        copies(*what, guarded("start", 1))

    def receive(*what, layers=(1, -1, 0)):
        copies(*what, guarded("wait_recv", -1), layers)

    def sent(*what):
        copies(*what, guarded("wait_send", 1))

    opening = (0, first, first_edge, geo_rows + rows)
    pl.semaphore_wait(barrier, devices - 1)
    send(*opening)

    shape = (slots, slots)
    eye = lax.broadcasted_iota(jnp.int32, shape, 0) == lax.broadcasted_iota(jnp.int32, shape, 1)

    @pl.loop(0, cells)
    def _(cell):
        i, j = cell // cells_y, cell % cells_y
        for c in range(4):
            row = first[1, i + 1, pl.ds(c * cells_y + j, 1), :]
            column = jnp.sum(jnp.where(eye, row, 0.0), axis=1, keepdims=True)
            local[cell, c] = jnp.broadcast_to(column, shape)

    def row_at(q, y, base, own_rows, edge_base, edge_rows):
        if y < 0:
            return own_rows + edge_base + 2 * q + 1
        if y >= cells_y:
            return own_rows + (sides - 1) * edge_rows + edge_base + 2 * q
        return base + q * cells_y + y

    geo_rule = (0, geo_rows + rows, 0, 12)
    start_rule = (geo_rows, geo_rows + rows, 8, 12)
    field_rule = (0, rows, 0, 4)

    def inside(i):
        return [1, 2 - 2 * i] if cells_x == 2 else [1]

    def outside(i):
        return [2 * i] if cells_x == 2 else [0, 2]

    def in_block(j, k):
        return 0 <= j + k - 1 < cells_y

    def couple(i, j, dz, dx, k):
        cell = i * cells_y + j
        tile = first.at[dz, i + dx]

        def line(q):
            at = row_at(q, j + k - 1, *geo_rule)
            return tile[at : at + 1, :]

        bz = line(0) + (jnp.asarray(dz, jnp.int32) - 1).astype(jnp.float32)
        bx = line(1) + (jnp.asarray(dx, jnp.int32) - 1).astype(jnp.float32)
        by = line(2) + (k - 1.0)
        bs = line(3)
        for part in range(slots // CHUNK):
            span = pl.ds(part * CHUNK, CHUNK)
            ez = bz - local[cell, 0, span]
            ex = bx - local[cell, 1, span]
            ey = by - local[cell, 2, span]
            squared = ez * ez + ex * ex + ey * ey
            fraction = squared * lax.rsqrt(jnp.maximum(squared, 1e-30))
            reach = jnp.maximum(1.0 - fraction, 0.0)
            reach = reach * reach
            factor = coulomb_factor / cell_edge
            taper = reach * reach * (4.0 * factor * fraction + factor)
            pair[cell, (dz * 3 + dx) * 3 + k, span] = taper * lax.rsqrt(
                squared + (local[cell, 3, span] + bs)
            )

    def build():
        @pl.loop(0, cells_x)
        def _(i):
            for dx in inside(i):
                for j in range(cells_y):
                    for k in range(3):
                        if in_block(j, k):
                            couple(i, j, 1, dx, k)

        receive(*opening, layers=(0,))

        @pl.loop(0, cells_x)
        def _(i):
            for dx in outside(i):
                for j in range(cells_y):
                    for k in range(3):
                        couple(i, j, 1, dx, k)
            for dx in inside(i):
                for j in range(cells_y):
                    for k in range(3):
                        if not in_block(j, k):
                            couple(i, j, 1, dx, k)

        receive(*opening, layers=(1, -1))

        @pl.loop(0, cells_x)
        def _(i):
            @pl.loop(0, 6)
            def _(plane):
                dz, dx = 2 * (plane // 3), plane % 3
                for j in range(cells_y):
                    for k in range(3):
                        couple(i, j, dz, dx, k)

    def add_pairs(buffer, rule, i, j, total, planes, chosen):
        for dz, dx in planes:
            for k in range(3):
                if not chosen(dz, dx, k):
                    continue
                tile = buffer.at[dz, i + dx]
                block = pair[i * cells_y + j, (dz * 3 + dx) * 3 + k]
                for s in range(2):
                    at = row_at(s, j + k - 1, *rule)
                    total[s] = total[s] + block * tile[at : at + 1, :]
        return total

    def operate_own(buffer, rule):
        @pl.loop(0, cells_x)
        def _(i):
            for j in range(cells_y):
                total = [jnp.zeros(shape, jnp.float32) for _ in range(2)]
                total = add_pairs(
                    buffer, rule, i, j, total,
                    [(1, dx) for dx in inside(i)], lambda dz, dx, k: in_block(j, k),
                )
                for s in range(2):
                    sums[i, s * cells_y + j] = total[s]

    def operate_rest(buffer, rule, field):
        @pl.loop(0, cells_x)
        def _(i):
            for j in range(cells_y):
                total = [sums[i, s * cells_y + j] for s in range(2)]
                total = add_pairs(
                    buffer, rule, i, j, total,
                    [(1, dx) for dx in inside(i)], lambda dz, dx, k: not in_block(j, k),
                )
                total = add_pairs(
                    buffer, rule, i, j, total,
                    [(1, dx) for dx in outside(i)]
                    + [(dz, dx) for dz in (0, 2) for dx in range(3)],
                    lambda dz, dx, k: True,
                )
                for s in range(2):
                    sums[i, s * cells_y + j] = total[s]

        out = []
        for i in range(cells_x):
            lines = []
            for row in range(rows):
                column = jnp.sum(sums[i, row], axis=1, keepdims=True)
                lines.append(jnp.sum(jnp.where(eye, column, 0.0), axis=0, keepdims=True))
            out.append(occ[i] * (stiff[i] * field[i] + jnp.concatenate(lines, axis=0)))
        return out

    tile_shape = (rows, slots)
    lane = lax.broadcasted_iota(jnp.int32, tile_shape, 1)
    second = lax.broadcasted_iota(jnp.int32, tile_shape, 0) >= cells_y
    slot_of = lane - jnp.where(second, 8, 0)

    def part_copy(stage, peer, slot):
        return pltpu.make_async_remote_copy(
            src_ref=mine.at[stage],
            dst_ref=parts.at[stage, slot],
            send_sem=part_send.at[stage],
            recv_sem=part_recv.at[stage],
            device_id=peer,
            device_id_type=MESH,
        )

    def start_sums(stage, quantities):
        packed = jnp.zeros(tile_shape, jnp.float32)
        for k, quantity in enumerate(quantities):
            column = jnp.sum(functools.reduce(jnp.add, quantity), axis=1, keepdims=True)
            packed = jnp.where(slot_of == k, column, packed)
        mine[stage] = jnp.sum(packed, axis=0, keepdims=True)
        each_peer(lambda peer, slot: part_copy(stage, peer, slot).start())

    def finish_sums(stage, count):
        everything = parts.at[stage]
        pltpu.make_async_copy(everything, everything, part_recv.at[stage]).wait()
        row = mine[stage] + jnp.sum(parts[stage], axis=0)
        pltpu.make_async_copy(everything, everything, part_send.at[stage]).wait()
        return [
            jnp.where(
                second,
                jnp.broadcast_to(row[:, 8 + k : 9 + k], tile_shape),
                jnp.broadcast_to(row[:, k : k + 1], tile_shape),
            )
            for k in range(count)
        ]

    span = range(cells_x)

    def exchange_and_operate(stage, field, meanwhile=None):
        buffer, edge = fields.at[stage - 1], edges.at[stage - 1]
        for i in span:
            buffer[1, i + 1, :rows] = field[i]
            pieces = [field[i][:cells_y], field[i][cells_y:]]
            edge[i] = jnp.concatenate([end for v in pieces for end in ends(v)], axis=0)
        what = (stage, buffer, edge, rows)
        send(*what)
        if meanwhile is not None:
            meanwhile()
        operate_own(buffer, field_rule)
        receive(*what)
        out = operate_rest(buffer, field_rule, field)
        sent(*what)
        return out

    build()
    operate_own(first, start_rule)
    image = operate_rest(first, start_rule, x)
    sent(*opening)
    r = [rhs[i] - image[i] for i in span]
    w = exchange_and_operate(1, r)

    p = s = z = None
    for stage in range(ITERS):
        quantities = [[r[i] * r[i] for i in span], [w[i] * r[i] for i in span]]
        last = stage == ITERS - 1
        if last:
            quantities += [x, r, p]
        go = functools.partial(start_sums, stage, quantities)
        n = go() if last else exchange_and_operate(stage + 2, w, go)
        found = finish_sums(stage, len(quantities))
        gamma, delta = found[:2]
        if stage == 0:
            beta = None
            alpha = gamma / delta
            p, s, z = r, w, n
        else:
            beta = gamma / gamma_before
            alpha = gamma / (delta - beta * gamma / alpha)
            p = [r[i] + beta * p[i] for i in span]
            s = [w[i] + beta * s[i] for i in span]
            if not last:
                z = [n[i] + beta * z[i] for i in span]
        gamma_before = gamma
        x = [x[i] + alpha * p[i] for i in span]
        r = [r[i] - alpha * s[i] for i in span]
        if not last:
            w = [w[i] - alpha * z[i] for i in span]
    totals = found[2] + alpha * (found[3] + beta * found[4])
    ratio = totals[:cells_y] / totals[cells_y:]
    for i in span:
        charges[0, i] = x[i][:cells_y] - ratio * x[i][cells_y:]
        residuals[0, 0, i] = r[i][:cells_y]
        residuals[1, 0, i] = r[i][cells_y:]


def per_device(sizes, *arrays):
    type_ids = arrays[1]
    cells_x, cells_y, slots = type_ids.shape[1:]
    cells = cells_x * cells_y
    rows = 2 * cells_y
    devices = sizes[0] * sizes[1] * sizes[2]
    dys = (0, 1) if sizes[2] == 2 else (0, 1, -1)
    messages = 9 * len(dys) - 1
    halo = (3, cells_x + 2)
    sides = len(dys) - 1
    vmem = pl.BlockSpec(memory_space=pltpu.VMEM)
    return pl.pallas_call(
        functools.partial(kernel, sizes, dys),
        out_shape=(
            jax.ShapeDtypeStruct(type_ids.shape, jnp.float32),
            jax.ShapeDtypeStruct((2,) + type_ids.shape, jnp.float32),
        ),
        in_specs=[pl.BlockSpec(memory_space=pltpu.HBM)] * 7,
        out_specs=(vmem, vmem),
        scratch_shapes=[
            *(pltpu.VMEM(array.shape, array.dtype) for array in arrays[:4]),
            *(pltpu.SMEM(array.shape, array.dtype) for array in arrays[4:]),
            pltpu.VMEM(halo + (6 * cells_y + 12 * sides, slots), jnp.float32),
            pltpu.VMEM((ITERS,) + halo + (rows + 4 * sides, slots), jnp.float32),
            pltpu.VMEM((cells_x, 12, slots), jnp.float32),
            pltpu.VMEM((ITERS, cells_x, 4, slots), jnp.float32),
            pltpu.VMEM((cells, 27, slots, slots), jnp.float32),
            pltpu.VMEM((cells, 4, slots, slots), jnp.float32),
            pltpu.VMEM((cells_x, rows, slots, slots), jnp.float32),
            pltpu.VMEM((ITERS, devices - 1, 1, slots), jnp.float32),
            pltpu.VMEM((ITERS, 1, slots), jnp.float32),
            pltpu.SemaphoreType.DMA((len(arrays),)),
            pltpu.SemaphoreType.DMA((ITERS + 1, messages)),
            pltpu.SemaphoreType.DMA((ITERS + 1, messages)),
            pltpu.SemaphoreType.DMA((ITERS,)),
            pltpu.SemaphoreType.DMA((ITERS,)),
        ],
        compiler_params=pltpu.CompilerParams(
            collective_id=0, has_side_effects=True, vmem_limit_bytes=48 * 1024 * 1024
        ),
    )(*arrays)


def solution(mesh):
    sizes = tuple(mesh.shape[name] for name in AXES)
    in_specs = (
        P(None, "gz", "gx", "gy", None),
        P("gz", "gx", "gy", None),
        P("gz", "gx", "gy", None),
        P(None, "gz", "gx", "gy", None),
        P(),
        P(),
        P(),
    )
    out_specs = (P("gz", "gx", "gy", None), P(None, "gz", "gx", "gy", None))
    return jax.shard_map(
        functools.partial(per_device, sizes),
        mesh=mesh,
        in_specs=in_specs,
        out_specs=out_specs,
        check_vma=False,
    )
```

time: 69.3 us -> 61.4 us (0.89)
  Pallas kernels: 62.3 us -> 54.4 us
    pallas_call x1, Pallas kernels: 62.3 us -> 54.4 us  [per_device(): pl.pallas_call(functools.partial(kernel, sizes, dys), out_shape=(jax.Shap...]
where the time goes in v1:
time: 61.4 us; the launch traced here: 61 us
  Pallas kernels  54.4 us (89%)
  local copies, waits for them, and re-layouts  5.93 us (10%)
  between operations  0.66 us (1%)
    pallas_call x1, Pallas kernels, per_device(): pl.pallas_call(functools.partial(kernel, sizes, dys), out_shape=(jax.Shap...  54.4 us
    unnamed x16, local copies, waits for them, and re-layouts  5.93 us

profile of v1, /device:TPU:0, one launch (start us, length us, event | category | flops | bytes accessed | tf_op | source)
XLA Modules:
  0.0 61.0 jit_solution(4841944958242069504)
XLA Ops:
  0.6 0.0 copy-start
  0.6 0.7 %copy-done = f32[3,1,2,4,128]{4,3,2,1,0:T(4,128)S(1)} copy-done((f32[3,1,2,4,128]{4,3,2,1,0:T(4,128)S(1)}, f32[3,1,2,4,128]{4,3,2,1,0:T(4,128)}, u32[]{:S(2)}) %copy-start) | copy-done | bytes 12312
  1.3 0.0 copy-start.1
  1.3 0.7 %copy-done.1 = f32[2,1,2,4,128]{4,3,2,1,0:T(4,128)S(1)} copy-done((f32[2,1,2,4,128]{4,3,2,1,0:T(4,128)S(1)}, f32[2,1,2,4,128]{4,3,2,1,0:T(4,128)}, u32[]{:S(2)}) %copy-start.1) | copy-done | bytes 8216
  2.0 0.0 copy-start.2
  2.0 0.7 %copy-done.2 = s32[1,2,4,128]{3,2,1,0:T(4,128)S(1)} copy-done((s32[1,2,4,128]{3,2,1,0:T(4,128)S(1)}, s32[1,2,4,128]{3,2,1,0:T(4,128)}, u32[]{:S(2)}) %copy-start.2) | copy-done | bytes 4120
  2.7 0.0 copy-start.3
  2.7 0.7 %copy-done.3 = s32[1,2,4,128]{3,2,1,0:T(4,128)S(1)} copy-done((s32[1,2,4,128]{3,2,1,0:T(4,128)S(1)}, s32[1,2,4,128]{3,2,1,0:T(4,128)}, u32[]{:S(2)}) %copy-start.3) | copy-done | bytes 4120
  3.4 0.0 copy-start.4
  3.4 0.7 %copy-done.4 = f32[3]{0:T(128)S(1)} copy-done((f32[3]{0:T(128)S(1)}, f32[3]{0:T(128)}, u32[]{:S(2)}) %copy-start.4) | copy-done | bytes 36
  4.1 0.0 copy-start.5
  4.1 0.7 %copy-done.5 = f32[3]{0:T(128)S(1)} copy-done((f32[3]{0:T(128)S(1)}, f32[3]{0:T(128)}, u32[]{:S(2)}) %copy-start.5) | copy-done | bytes 36
  4.7 0.0 copy-start.6
  4.7 0.7 %copy-done.6 = f32[3]{0:T(128)S(1)} copy-done((f32[3]{0:T(128)S(1)}, f32[3]{0:T(128)}, u32[]{:S(2)}) %copy-start.6) | copy-done | bytes 36
  5.4 54.4 %shard_map.86 = (f32[1,2,4,128]{3,2,1,0:T(4,128)S(1)}, f32[2,1,2,4,128]{4,3,2,1,0:T(4,128)S(1)}) custom-call(f32[3,1,2,4,128]{4,3,2,1,0:T(4,128)S(1)} %copy-done, s32[1,2,4,128]{3,2,1,0:T(4,128)S(1)} %copy-done.2, s32[1,2,4,128]{3,2,1,0:T(4,128)S(1)} %copy-done.3, f32[2,1,2,4,128]{4,3,2,1,0:T(4,128)S(1)} %copy-done.1, f32[3]{0:T(128)S(1)} %copy-done.4, ...), custom_call_target="tpu_custom_call" | custom-call | tf_op jit(solution)/shard_map/pallas_call | solution.py:421
  59.8 0.6 copy.11
  60.4 0.6 copy.12
Async XLA Ops:
  0.6 0.7 %copy-start = (f32[3,1,2,4,128]{4,3,2,1,0:T(4,128)S(1)}, f32[3,1,2,4,128]{4,3,2,1,0:T(4,128)}, u32[]{:S(2)}) copy-start(f32[3,1,2,4,128]{4,3,2,1,0:T(4,128)} %offsets_in.1) | copy-start | bytes 36868
  1.3 0.7 %copy-start.1 = (f32[2,1,2,4,128]{4,3,2,1,0:T(4,128)S(1)}, f32[2,1,2,4,128]{4,3,2,1,0:T(4,128)}, u32[]{:S(2)}) copy-start(f32[2,1,2,4,128]{4,3,2,1,0:T(4,128)} %prior_in.1) | copy-start | bytes 24580
  2.0 0.7 %copy-start.2 = (s32[1,2,4,128]{3,2,1,0:T(4,128)S(1)}, s32[1,2,4,128]{3,2,1,0:T(4,128)}, u32[]{:S(2)}) copy-start(s32[1,2,4,128]{3,2,1,0:T(4,128)} %type_ids_in.1) | copy-start | bytes 12292
  2.7 0.7 %copy-start.3 = (s32[1,2,4,128]{3,2,1,0:T(4,128)S(1)}, s32[1,2,4,128]{3,2,1,0:T(4,128)}, u32[]{:S(2)}) copy-start(s32[1,2,4,128]{3,2,1,0:T(4,128)} %occupied_in.1) | copy-start | bytes 12292
  3.4 0.7 %copy-start.4 = (f32[3]{0:T(128)S(1)}, f32[3]{0:T(128)}, u32[]{:S(2)}) copy-start(f32[3]{0:T(128)} %electro_in.1) | copy-start | bytes 40
  4.1 0.7 %copy-start.5 = (f32[3]{0:T(128)S(1)}, f32[3]{0:T(128)}, u32[]{:S(2)}) copy-start(f32[3]{0:T(128)} %hardness_in.1) | copy-start | bytes 40
  4.7 0.7 %copy-start.6 = (f32[3]{0:T(128)S(1)}, f32[3]{0:T(128)}, u32[]{:S(2)}) copy-start(f32[3]{0:T(128)} %shielding_in.1) | copy-start | bytes 40

commit v2 on v1

--- a/solution.py
+++ b/solution.py
@@ -424,7 +424,7 @@
             jax.ShapeDtypeStruct(type_ids.shape, jnp.float32),
             jax.ShapeDtypeStruct((2,) + type_ids.shape, jnp.float32),
         ),
-        in_specs=[pl.BlockSpec(memory_space=pltpu.HBM)] * 7,
+        in_specs=[pl.BlockSpec(memory_space=pl.ANY)] * 7,
         out_specs=(vmem, vmem),
         scratch_shapes=[
             *(pltpu.VMEM(array.shape, array.dtype) for array in arrays[:4]),
@@ -445,7 +445,7 @@
             pltpu.SemaphoreType.DMA((ITERS,)),
         ],
         compiler_params=pltpu.CompilerParams(
-            collective_id=0, has_side_effects=True, vmem_limit_bytes=48 * 1024 * 1024
+            collective_id=0, has_side_effects=True, vmem_limit_bytes=60 * 1024 * 1024
         ),
     )(*arrays)
 

time: 61.4 us -> 57.8 us (0.941)
  local copies, waits for them, and re-layouts: 5.93 us -> 1.88 us
    unnamed x16 -> x4, local copies, waits for them, and re-layouts: 5.93 us -> 1.88 us
where the time goes in v2:
time: 57.8 us; the launch traced here: 57.5 us
  Pallas kernels  55 us (95%)
  local copies, waits for them, and re-layouts  1.88 us (3%)
  between operations  0.65 us (1%)
    pallas_call x1, Pallas kernels, per_device(): pl.pallas_call(functools.partial(kernel, sizes, dys), out_shape=(jax.Shap...  55 us
    unnamed x4, local copies, waits for them, and re-layouts  1.88 us

profile of v2, /device:TPU:0, one launch (start us, length us, event | category | flops | bytes accessed | tf_op | source)
XLA Modules:
  0.0 57.5 jit_solution(16180721194186610229)
XLA Ops:
  0.6 55.0 %shard_map.86 = (f32[1,2,4,128]{3,2,1,0:T(4,128)}, f32[2,1,2,4,128]{4,3,2,1,0:T(4,128)}) custom-call(f32[3,1,2,4,128]{4,3,2,1,0:T(4,128)} %offsets_in.1, s32[1,2,4,128]{3,2,1,0:T(4,128)} %type_ids_in.1, s32[1,2,4,128]{3,2,1,0:T(4,128)} %occupied_in.1, f32[2,1,2,4,128]{4,3,2,1,0:T(4,128)} %prior_in.1, f32[3]{0:T(128)} %electro_in.1, f32[3]{0:T(128)} %hardness_in.1, ...), custom_call_target="tpu_custom_call" | custom-call | tf_op jit(solution)/shard_map/pallas_call | solution.py:421
  55.6 0.0 copy-start
  55.6 1.3 %copy.11 = f32[1,2,4,128]{3,2,1,0:T(4,128)} copy(f32[1,2,4,128]{3,2,1,0:T(4,128)} %get-tuple-element.4) | data formatting | bytes 8192
  56.9 0.0 copy-done
  56.9 0.6 %copy.12 = f32[2,1,2,4,128]{4,3,2,1,0:T(4,128)} copy(f32[2,1,2,4,128]{4,3,2,1,0:T(4,128)S(1)} %copy-done) | data formatting | bytes 16384
Async XLA Ops:
  55.6 1.3 %copy-start = (f32[2,1,2,4,128]{4,3,2,1,0:T(4,128)S(1)}, f32[2,1,2,4,128]{4,3,2,1,0:T(4,128)}, u32[]{:S(2)}) copy-start(f32[2,1,2,4,128]{4,3,2,1,0:T(4,128)} %get-tuple-element.5) | copy-start | bytes 24580
